TPU v7x, 32 devices: a whole 2x2x4 slice. The times are simulated.
32 devices in a mesh: tm: 8 (over z, core), dp: 4 (over y, x).
Axes of the slice: x: 2, y: 2, z: 4, core: 2. Of those that a mesh axis runs over, the one named last changes fastest.
Arguments:
- encoded: bfloat16 [512, 80, 1024], P('dp', 'tm'), may hold values from -6 to 6
- queries: bfloat16 [512, 32, 1024], P(('dp', 'tm')), may hold values from -200 to 200
- cotangent: bfloat16 [512, 32, 1024], P(('dp', 'tm')), may hold values from -0.08886719 to 0.08886719
- lengths: int32 [512], P(('dp', 'tm')), may hold values from 2 to 80
- key_weight: bfloat16 [1024, 1024], replicated, may hold values from -0.1875 to 0.1875
- value_weight: bfloat16 [1024, 1024], replicated, may hold values from -0.1875 to 0.1875
Outputs:
- context: bfloat16 [512, 32, 1024], P(('dp', 'tm'))
- key_grad: float32 [1024, 1024], replicated
- value_grad: float32 [1024, 1024], replicated
Inputs may be any that keep to these rules, and one draw needn't show every extreme that they name: Sequence b attends only to source positions below lengths[b].
All inputs are finite; a program needn't handle non-finite values.
Results may differ from a plain program's by a relative error of at most 0.0069.
Values may be sent and summed in bfloat16 or wider, within the bound.
A program may use at most 128 MiB of HBM per device.

v0:
```python
import math
import jax
import jax.numpy as jnp
from jax import lax
from jax.sharding import PartitionSpec as P


def attend(queries, key_rows, value_rows, lengths, cotangent):
    score_scale = 1.0 / math.sqrt(queries.shape[-1])
    scores = (
        jnp.einsum("btd,bsd->bts", queries, key_rows, preferred_element_type=jnp.float32)
        * score_scale
    )
    positions = jnp.arange(key_rows.shape[1], dtype=jnp.int32)
    in_range = positions[None, None, :] < lengths[:, None, None]
    scores = jnp.where(in_range, scores, -1e30)
    row_max = jnp.max(scores, axis=-1, keepdims=True)
    weights = jnp.exp(scores - row_max)
    probabilities = weights / jnp.sum(weights, axis=-1, keepdims=True)
    probs_low = probabilities.astype(jnp.bfloat16)
    context = jnp.einsum(
        "bts,bsd->btd", probs_low, value_rows, preferred_element_type=jnp.float32
    ).astype(jnp.bfloat16)
    grad_probs = jnp.einsum(
        "btd,bsd->bts", cotangent, value_rows, preferred_element_type=jnp.float32
    )
    grad_scores = probabilities * (
        grad_probs - jnp.sum(probabilities * grad_probs, axis=-1, keepdims=True)
    )
    grad_low = grad_scores.astype(jnp.bfloat16)
    grad_values = jnp.einsum(
        "bts,btd->bsd", probs_low, cotangent, preferred_element_type=jnp.float32
    ).astype(jnp.bfloat16)
    grad_keys = (
        jnp.einsum("bts,btd->bsd", grad_low, queries, preferred_element_type=jnp.float32)
        * score_scale
    ).astype(jnp.bfloat16)
    return (context, grad_keys, grad_values)


def project(flattened, weight_matrix, shape):
    return (
        jnp.dot(flattened, weight_matrix, preferred_element_type=jnp.float32)
        .astype(jnp.bfloat16)
        .reshape(shape)
    )


def weight_term(flattened, gradient):
    model_width = flattened.shape[1]
    return lax.dot_general(
        flattened,
        gradient.reshape(-1, model_width),
        (((0,), (0,)), ((), ())),
        preferred_element_type=jnp.float32,
    )


def body(encoded, queries, cotangent, lengths, key_weight, value_weight):
    model_width = encoded.shape[2]
    regrouped = lax.all_to_all(encoded, "tm", split_axis=0, concat_axis=1, tiled=True)
    flattened = regrouped.reshape(-1, model_width)
    key_rows = project(flattened, key_weight, regrouped.shape)
    value_rows = project(flattened, value_weight, regrouped.shape)
    context, grad_keys, grad_values = attend(queries, key_rows, value_rows, lengths, cotangent)
    key_grad = weight_term(flattened, grad_keys)
    value_grad = weight_term(flattened, grad_values)
    key_grad, value_grad = lax.psum((key_grad, value_grad), ("tm", "dp"))
    return (context, key_grad, value_grad)


def solution(mesh):
    return jax.shard_map(
        body,
        mesh=mesh,
        in_specs=(
            P("dp", "tm", None),
            P(("dp", "tm"), None, None),
            P(("dp", "tm"), None, None),
            P(("dp", "tm")),
            P(),
            P(),
        ),
        out_specs=(P(("dp", "tm"), None, None), P(), P()),
        check_vma=False,
    )
```

profile of v0, /device:TPU:0, one launch (start us, length us, event | category | flops | bytes accessed | tf_op | source)
XLA Modules:
  0.0 355.5 jit_solution(7292842336370048144)
XLA Ops:
  7.2 0.0 copy-start
  7.2 5.5 %copy.14 = bf16[128,10,1024]{2,1,0:T(8,128)(2,1)} copy(bf16[128,10,1024]{2,0,1:T(8,128)(2,1)} %param.6) | data formatting | bytes 5242880 | tf_op args[0]
  12.7 0.0 copy-start.5
  12.7 6.5 %all-to-all-start = ((bf16[128,10,1024]{2,1,0:T(8,128)(2,1)}), bf16[128,10,1024]{2,1,0:T(8,128)(2,1)}, u32[]{:S(2)}, u32[]{:S(2)}) async-start(bf16[128,10,1024]{2,1,0:T(8,128)(2,1)} %copy.14), calls=%async_computation | async-start | bytes 8388608 | tf_op jit(solution)/shard_map/all_to_all | solution.py:61
  19.2 0.0 all-reduce.3.cloned.1.call-start
  19.2 0.0 copy-done.5
  19.3 0.1 iota_compare_fusion
  19.3 94.0 %all-to-all-done = bf16[128,10,1024]{2,1,0:T(8,128)(2,1)} async-done(((bf16[128,10,1024]{2,1,0:T(8,128)(2,1)}), bf16[128,10,1024]{2,1,0:T(8,128)(2,1)}, u32[]{:S(2)}, u32[]{:S(2)}) %all-to-all-start) | async-done | bytes 2621472 | tf_op jit(solution)/shard_map/all_to_all | solution.py:61
  113.3 5.0 %copy.19 = bf16[8,16,10,1024]{3,2,0,1:T(8,128)(2,1)} copy(bf16[8,16,10,1024]{3,2,1,0:T(8,128)(2,1)} %bitcast) | data formatting | bytes 5242880 | tf_op jit(solution)/shard_map/all_to_all | solution.py:61
  118.3 6.1 %reshape.46 = bf16[1280,1024]{1,0:T(8,128)(2,1)} reshape(bf16[16,8,10,1024]{3,2,1,0:T(8,128)(2,1)} %bitcast.35) | data formatting | bytes 5242880 | tf_op jit(solution)/shard_map/reshape | solution.py:62
  124.5 0.0 copy-done
  124.5 0.0 copy-start.3
  124.5 0.0 copy-start.6
  124.5 6.1 %convolution_convert_fusion = bf16[1280,1024]{1,0:T(8,128)(2,1)} fusion(bf16[1280,1024]{1,0:T(8,128)(2,1)} %reshape.46, bf16[1024,1024]{1,0:T(8,128)(2,1)S(1)} %copy-done), kind=kOutput, calls=%fused_computation.3 | convolution fusion | flops 2685665280 | bytes 7340032 | tf_op jit(solution)/shard_map/dot_general | solution.py:43
  130.6 0.0 copy-done.3
  130.6 0.0 copy-done.6
  130.6 3.1 convolution_convert_fusion.1
  133.7 0.0 copy-done.1
  133.7 0.8 fusion.4
  134.6 0.9 fusion.8
  135.4 4.6 %convolution_convert_fusion.2 = bf16[16,80,1024]{2,1,0:T(8,128)(2,1)} fusion(bf16[16,32,1024]{2,1,0:T(8,128)(2,1)} %param.8, f32[16,32]{1,0:T(8,128)S(1)} %get-tuple-element.14, f32[16,32,80]{2,1,0:T(8,128)S(1)} %fusion.4), kind=kOutput, calls=%fused_computation.7 | convolution fusion | flops 85320272 | bytes 3835904 | tf_op jit(solution)/shard_map/bts,btd->bsd/dot_general | solution.py:31
  140.0 3.6 %multiply_reduce_fusion = (f32[16,32]{1,0:T(8,128)S(1)}, f32[16,32,80]{2,1,0:T(8,128)}) fusion(f32[16,32,80]{2,1,0:T(8,128)} %get-tuple-element.15, f32[16,32]{1,0:T(8,128)S(1)} %get-tuple-element.14, bf16[16,80,1024]{2,1,0:T(8,128)(2,1)} %bitcast.36, bf16[16,32,1024]{2,1,0:T(8,128)(2,1)} %param.8), kind=kOutput, calls=%fused_computation.16 | convolution fusion | flops 84008448 | bytes 4001792 | tf_op jit(solution)/shard_map/btd,bsd->bts/dot_general | solution.py:24
  143.6 4.1 %multiply_convert_fusion = bf16[16,80,1024]{2,1,0:T(8,128)(2,1)} fusion(bf16[16,32,1024]{2,1,0:T(8,128)(2,1)S(1)} %copy-done.1, f32[16,32,80]{2,1,0:T(8,128)} %get-tuple-element.17, f32[16,32]{1,0:T(8,128)S(1)} %get-tuple-element.16, f32[16,32]{1,0:T(8,128)S(1)} %get-tuple-element.14, f32[16,32,80]{2,1,0:T(8,128)S(1)} %fusion.4), kind=kOutput, calls=%fused_computation.1 | convolution fusion | flops 86712912 | bytes 4001792 | tf_op jit(solution)/shard_map/bts,btd->bsd/dot_general | solution.py:35
  147.8 7.6 %convolution_bitcast_fusion.1 = f32[1024,1024]{0,1:T(8,128)} fusion(bf16[1280,1024]{1,0:T(8,128)(2,1)} %bitcast.40, bf16[1280,1024]{1,0:T(8,128)(2,1)} %reshape.46), kind=kOutput, calls=%fused_computation.6 | convolution fusion | flops 2684354560 | bytes 9437184 | tf_op jit(solution)/shard_map/dot_general | solution.py:51
  155.4 0.0 copy-done.2
  155.4 0.0 copy-done.4
  155.4 4.4 %convolution_bitcast_fusion = f32[1024,1024]{0,1:T(8,128)} fusion(bf16[1280,1024]{1,0:T(8,128)(2,1)S(1)} %bitcast.38, bf16[1280,1024]{1,0:T(8,128)(2,1)S(1)} %copy-done.4), kind=kOutput, calls=%fused_computation.5 | convolution fusion | flops 2684354560 | bytes 9437184 | tf_op jit(solution)/shard_map/dot_general | solution.py:51
  159.8 0.0 all-reduce.3.cloned.1.call-update
  159.9 3.8 %convolution_convert_fusion.3 = bf16[16,32,1024]{2,1,0:T(8,128)(2,1)} fusion(bf16[16,80,1024]{2,1,0:T(8,128)(2,1)} %bitcast.37, f32[16,32]{1,0:T(8,128)S(1)} %get-tuple-element.14, f32[16,32,80]{2,1,0:T(8,128)S(1)} %fusion.4), kind=kOutput, calls=%fused_computation.8 | convolution fusion | flops 84533840 | bytes 3835904 | tf_op jit(solution)/shard_map/bts,bsd->btd/dot_general | solution.py:21
  163.7 174.3 %all-reduce.3.cloned.1.call-done = (f32[1024,1024]{0,1:T(8,128)}, f32[1024,1024]{0,1:T(8,128)}) async-done(((f32[1024,1024]{0,1:T(8,128)}, f32[1024,1024]{0,1:T(8,128)}), (f32[1024,1024]{0,1:T(8,128)}, f32[1024,1024]{0,1:T(8,128)})) %all-reduce.3.cloned.1.call-update) | async-done | bytes 8388624 | tf_op jit(solution)/shard_map/psum | solution.py:68
  338.0 5.3 %copy.16 = f32[1024,1024]{1,0:T(8,128)} copy(f32[1024,1024]{0,1:T(8,128)} %get-tuple-element.12) | data formatting | bytes 8388608
  343.4 5.3 %copy.17 = f32[1024,1024]{1,0:T(8,128)} copy(f32[1024,1024]{0,1:T(8,128)} %get-tuple-element.13) | data formatting | bytes 8388608
  (3 shorter events, 0.0 us)
Async XLA Ops:
  7.2 117.3 %copy-start = (bf16[1024,1024]{1,0:T(8,128)(2,1)S(1)}, bf16[1024,1024]{1,0:T(8,128)(2,1)}, u32[]{:S(2)}) copy-start(bf16[1024,1024]{1,0:T(8,128)(2,1)} %param.11) | copy-start | bytes 6291460
  12.7 6.5 %copy-start.5 = (s32[16]{0:T(128)S(1)}, s32[16]{0:T(128)}, u32[]{:S(2)}) copy-start(s32[16]{0:T(128)} %param.9) | copy-start | bytes 196
  12.7 100.6 %all-to-all-start = ((bf16[128,10,1024]{2,1,0:T(8,128)(2,1)}), bf16[128,10,1024]{2,1,0:T(8,128)(2,1)}, u32[]{:S(2)}, u32[]{:S(2)}) async-start(bf16[128,10,1024]{2,1,0:T(8,128)(2,1)} %copy.14), calls=%async_computation | async-start | bytes 8388608 | tf_op jit(solution)/shard_map/all_to_all | solution.py:61
  19.2 318.8 %all-reduce.3.cloned.1.call-start = ((), (), s32[]{:S(2)}) async-start(), calls=%async_computation.1 | async-start | bytes 16777216 | tf_op jit(solution)/shard_map/psum | solution.py:68
  124.5 6.1 %copy-start.3 = (bf16[1280,1024]{1,0:T(8,128)(2,1)S(1)}, bf16[1280,1024]{1,0:T(8,128)(2,1)}, u32[]{:S(2)}) copy-start(bf16[1280,1024]{1,0:T(8,128)(2,1)} %reshape.46) | copy-start | bytes 7864324
  124.5 6.1 %copy-start.6 = (bf16[1024,1024]{1,0:T(8,128)(2,1)S(1)}, bf16[1024,1024]{1,0:T(8,128)(2,1)}, u32[]{:S(2)}) copy-start(bf16[1024,1024]{1,0:T(8,128)(2,1)} %param.10) | copy-start | bytes 6291460
  130.6 3.1 copy-start.1
  147.8 7.6 %copy-start.2 = (bf16[16,80,1024]{2,1,0:T(8,128)(2,1)S(1)}, bf16[16,80,1024]{2,1,0:T(8,128)(2,1)}, u32[]{:S(2)}) copy-start(bf16[16,80,1024]{2,1,0:T(8,128)(2,1)} %convolution_convert_fusion.2) | copy-start | bytes 7864324
  147.8 7.6 %copy-start.4 = (bf16[1280,1024]{1,0:T(8,128)(2,1)S(1)}, bf16[1280,1024]{1,0:T(8,128)(2,1)}, u32[]{:S(2)}) copy-start(bf16[1280,1024]{1,0:T(8,128)(2,1)} %reshape.46) | copy-start | bytes 7864324
Sparse Core Ops, SparseCore 0:
  160.0 177.9 all-reduce.2
where the time goes:
time: 356 us
  waiting for transfers between devices  268 us (75%)
  matrix products  38.3 us (11%)
  local copies, waits for them, and re-layouts  27.4 us (8%)
  between operations  14.1 us (4%)
  starting transfers between devices  6.52 us (2%)
    psum x1, waiting for transfers between devices, body(): key_grad, value_grad = lax.psum((key_grad, value_grad), ('tm', 'dp'))  174 us
    all_to_all x1, waiting for transfers between devices, body(): lax.all_to_all(encoded, 'tm', split_axis=0, concat_axis=1, tiled=True)  94 us
    unnamed x17, local copies, waits for them, and re-layouts  16.2 us
    dot_general x2, matrix products, weight_term(): lax.dot_general(flattened, gradient.reshape(-1, model_width), (((0,), (0,...  12.1 us
    dot_general x2, matrix products, project(): jnp.dot(flattened, weight_matrix, preferred_element_type=jnp.float32)  9.23 us
  transfers between devices with their start and end apart: 2, of which 2 were waited for; matrix products, arithmetic and copies ran while one was open for 1% of the time, Pallas kernels for 0%

commit v1 on v0

--- a/solution.py
+++ b/solution.py
@@ -65,7 +65,7 @@
     context, grad_keys, grad_values = attend(queries, key_rows, value_rows, lengths, cotangent)
     key_grad = weight_term(flattened, grad_keys)
     value_grad = weight_term(flattened, grad_values)
-    key_grad, value_grad = lax.psum((key_grad, value_grad), ("tm", "dp"))
+    key_grad, value_grad = jax.lax.psum(jax.lax.psum((key_grad, value_grad), "dp"), "tm")
     return (context, key_grad, value_grad)
 
 

time: 356 us -> 527 us (1.48)
  waiting for transfers between devices: 268 us -> 440 us
    psum x1 -> x2, waiting for transfers between devices: 174 us -> 346 us  [the longest x1 175 us: body(): jax.lax.psum(jax.lax.psum((key_grad, value_grad), 'dp'), 'tm')]
    unnamed x17 -> x21, local copies, waits for them, and re-layouts: 16.2 us -> 16.4 us
  transfers between devices with their start and end apart: 2 -> 3, of which waited for: 2 -> 3; matrix products, arithmetic and copies ran while one was open for 1% -> 1% of each run, Pallas kernels for 0% -> 0%
where the time goes in v1:
time: 527 us; the launch traced here: 526 us
  waiting for transfers between devices  440 us (83%)
  matrix products  35.2 us (7%)
  local copies, waits for them, and re-layouts  27.6 us (5%)
  between operations  14.1 us (3%)
  starting transfers between devices  6.56 us (1%)
    psum x1, waiting for transfers between devices, body(): jax.lax.psum(jax.lax.psum((key_grad, value_grad), 'dp'), 'tm')  175 us
    psum x1, waiting for transfers between devices, body(): jax.lax.psum((key_grad, value_grad), 'dp')  171 us
    all_to_all x1, waiting for transfers between devices, body(): lax.all_to_all(encoded, 'tm', split_axis=0, concat_axis=1, tiled=True)  94 us
    unnamed x21, local copies, waits for them, and re-layouts  16.4 us
    dot_general x2, matrix products, weight_term(): lax.dot_general(flattened, gradient.reshape(-1, model_width), (((0,), (0,...  12.1 us
  transfers between devices with their start and end apart: 3, of which 3 were waited for; matrix products, arithmetic and copies ran while one was open for 1% of the time, Pallas kernels for 0%

profile of v1, /device:TPU:0, one launch (start us, length us, event | category | flops | bytes accessed | tf_op | source)
XLA Modules:
  0.0 526.2 jit_solution(5877260115512305339)
XLA Ops:
  7.2 0.0 copy-start
  7.2 5.5 %copy.14 = bf16[128,10,1024]{2,1,0:T(8,128)(2,1)} copy(bf16[128,10,1024]{2,0,1:T(8,128)(2,1)} %param.6) | data formatting | bytes 5242880 | tf_op args[0]
  12.7 6.5 %all-to-all-start = ((bf16[128,10,1024]{2,1,0:T(8,128)(2,1)}), bf16[128,10,1024]{2,1,0:T(8,128)(2,1)}, u32[]{:S(2)}, u32[]{:S(2)}) async-start(bf16[128,10,1024]{2,1,0:T(8,128)(2,1)} %copy.14), calls=%async_computation | async-start | bytes 8388608 | tf_op jit(solution)/shard_map/all_to_all | solution.py:61
  19.2 0.0 all-reduce.7.cloned.1.call-start
  19.2 0.0 copy-done.7
  19.3 0.1 iota_compare_fusion
  19.3 94.0 %all-to-all-done = bf16[128,10,1024]{2,1,0:T(8,128)(2,1)} async-done(((bf16[128,10,1024]{2,1,0:T(8,128)(2,1)}), bf16[128,10,1024]{2,1,0:T(8,128)(2,1)}, u32[]{:S(2)}, u32[]{:S(2)}) %all-to-all-start) | async-done | bytes 2621472 | tf_op jit(solution)/shard_map/all_to_all | solution.py:61
  113.3 5.0 copy.19
  118.3 6.1 %reshape.46 = bf16[1280,1024]{1,0:T(8,128)(2,1)} reshape(bf16[16,8,10,1024]{3,2,1,0:T(8,128)(2,1)} %bitcast.35) | data formatting | bytes 5242880 | tf_op jit(solution)/shard_map/reshape | solution.py:62
  124.5 0.0 copy-done
  124.5 6.2 %convolution_convert_fusion = bf16[1280,1024]{1,0:T(8,128)(2,1)} fusion(bf16[1280,1024]{1,0:T(8,128)(2,1)} %reshape.46, bf16[1024,1024]{1,0:T(8,128)(2,1)S(1)} %copy-done), kind=kOutput, calls=%fused_computation.3 | convolution fusion | flops 2685665280 | bytes 7340032 | tf_op jit(solution)/shard_map/dot_general | solution.py:43
  130.6 0.0 copy-done.4
  130.7 0.0 copy-done.8
  130.7 3.1 convolution_convert_fusion.1
  133.8 0.0 copy-start.6
  133.8 0.0 copy-done.2
  133.8 0.8 fusion.4
  134.6 2.8 fusion.8
  137.4 0.0 copy-done.6
  137.4 3.4 convolution_convert_fusion.2
  140.8 2.6 multiply_reduce_fusion
  143.4 3.2 multiply_convert_fusion
  146.6 7.6 %convolution_bitcast_fusion.1 = f32[1024,1024]{0,1:T(8,128)} fusion(bf16[1280,1024]{1,0:T(8,128)(2,1)} %bitcast.40, bf16[1280,1024]{1,0:T(8,128)(2,1)} %reshape.46), kind=kOutput, calls=%fused_computation.6 | convolution fusion | flops 2684354560 | bytes 9437184 | tf_op jit(solution)/shard_map/dot_general | solution.py:51
  154.2 4.4 convolution_bitcast_fusion
  158.7 0.0 all-reduce.7.cloned.1.call-update
  158.7 0.0 all-reduce.5.cloned.1.call-start
  158.8 171.1 %all-reduce.7.cloned.1.call-done = (f32[1024,1024]{0,1:T(8,128)}, f32[1024,1024]{0,1:T(8,128)}) async-done(((f32[1024,1024]{0,1:T(8,128)}, f32[1024,1024]{0,1:T(8,128)}), (f32[1024,1024]{0,1:T(8,128)}, f32[1024,1024]{0,1:T(8,128)})) %all-reduce.7.cloned.1.call-update) | async-done | bytes 8388624 | tf_op jit(solution)/shard_map/psum | solution.py:68
  329.8 0.0 all-reduce.5.cloned.1.call-update
  329.9 3.8 convolution_convert_fusion.3
  333.7 174.8 %all-reduce.5.cloned.1.call-done = (f32[1024,1024]{0,1:T(8,128)}, f32[1024,1024]{0,1:T(8,128)}) async-done(((f32[1024,1024]{0,1:T(8,128)}, f32[1024,1024]{0,1:T(8,128)}), (f32[1024,1024]{0,1:T(8,128)}, f32[1024,1024]{0,1:T(8,128)})) %all-reduce.5.cloned.1.call-update) | async-done | bytes 8388624 | tf_op jit(solution)/shard_map/psum | solution.py:68
  508.5 5.3 %copy.16 = f32[1024,1024]{1,0:T(8,128)} copy(f32[1024,1024]{0,1:T(8,128)} %get-tuple-element.12) | data formatting | bytes 8388608
  513.9 5.5 %copy.17 = f32[1024,1024]{1,0:T(8,128)} copy(f32[1024,1024]{0,1:T(8,128)} %get-tuple-element.13) | data formatting | bytes 8388608
  (10 shorter events, 0.0 us)
Async XLA Ops:
  7.2 117.3 %copy-start = (bf16[1024,1024]{1,0:T(8,128)(2,1)S(1)}, bf16[1024,1024]{1,0:T(8,128)(2,1)}, u32[]{:S(2)}) copy-start(bf16[1024,1024]{1,0:T(8,128)(2,1)} %param.11) | copy-start | bytes 6291460
  12.7 6.5 %copy-start.7 = (s32[16]{0:T(128)S(1)}, s32[16]{0:T(128)}, u32[]{:S(2)}) copy-start(s32[16]{0:T(128)} %param.9) | copy-start | bytes 196
  12.7 100.6 %all-to-all-start = ((bf16[128,10,1024]{2,1,0:T(8,128)(2,1)}), bf16[128,10,1024]{2,1,0:T(8,128)(2,1)}, u32[]{:S(2)}, u32[]{:S(2)}) async-start(bf16[128,10,1024]{2,1,0:T(8,128)(2,1)} %copy.14), calls=%async_computation | async-start | bytes 8388608 | tf_op jit(solution)/shard_map/all_to_all | solution.py:61
  19.2 310.6 %all-reduce.7.cloned.1.call-start = ((), (), s32[]{:S(2)}) async-start(), calls=%async_computation.2 | async-start | bytes 16777216 | tf_op jit(solution)/shard_map/psum | solution.py:68
  124.5 6.2 %copy-start.4 = (bf16[1280,1024]{1,0:T(8,128)(2,1)S(1)}, bf16[1280,1024]{1,0:T(8,128)(2,1)}, u32[]{:S(2)}) copy-start(bf16[1280,1024]{1,0:T(8,128)(2,1)} %reshape.46) | copy-start | bytes 7864324
  124.5 6.2 %copy-start.8 = (bf16[1024,1024]{1,0:T(8,128)(2,1)S(1)}, bf16[1024,1024]{1,0:T(8,128)(2,1)}, u32[]{:S(2)}) copy-start(bf16[1024,1024]{1,0:T(8,128)(2,1)} %param.10) | copy-start | bytes 6291460
  130.7 3.1 copy-start.2
  133.8 3.6 copy-start.6
  146.6 7.6 %copy-start.3 = (bf16[16,80,1024]{2,1,0:T(8,128)(2,1)S(1)}, bf16[16,80,1024]{2,1,0:T(8,128)(2,1)}, u32[]{:S(2)}) copy-start(bf16[16,80,1024]{2,1,0:T(8,128)(2,1)} %convolution_convert_fusion.2) | copy-start | bytes 7864324
  146.6 7.6 %copy-start.5 = (bf16[1280,1024]{1,0:T(8,128)(2,1)S(1)}, bf16[1280,1024]{1,0:T(8,128)(2,1)}, u32[]{:S(2)}) copy-start(bf16[1280,1024]{1,0:T(8,128)(2,1)} %reshape.46) | copy-start | bytes 7864324
  158.7 349.8 %all-reduce.5.cloned.1.call-start = ((), (), s32[]{:S(2)}) async-start(), calls=%async_computation.1 | async-start | bytes 16777216 | tf_op jit(solution)/shard_map/psum | solution.py:68
  513.9 5.5 %copy-start.1 = (bf16[1024,1024]{1,0:T(8,128)(2,1)S(1)}, bf16[1024,1024]{1,0:T(8,128)(2,1)}, u32[]{:S(2)}) copy-start(bf16[1024,1024]{1,0:T(8,128)(2,1)} %param.11) | copy-start | bytes 6291460
Sparse Core Ops, SparseCore 0:
  158.8 170.9 all-reduce.6
  332.2 176.2 all-reduce.4
